TPU v7x, 32 devices: a whole 2x2x4 slice. The times are simulated.
32 devices in a mesh: seg: 8 (over z, core), head: 4 (over y, x).
Axes of the slice: x: 2, y: 2, z: 4, core: 2. Of those that a mesh axis runs over, the one named last changes fastest.
Arguments:
- inputs: bfloat16 [8, 256, 16384], P('seg', None, 'head'), may hold values from -6 to 6
- deltas: float32 [8, 256, 256], P('seg', 'head'), may hold values from 0.01 to 0.1
- rates: float32 [256], P('head'), may hold values from 0.001 to 2
- skips: float32 [256], P('head'), may hold values from 0.5 to 1.5
- writer: bfloat16 [8, 256, 1024], P('seg'), may hold values from -1.796875 to 1.796875
- reader: bfloat16 [8, 256, 1024], P('seg'), may hold values from -1.796875 to 1.796875
- grad_out: bfloat16 [8, 256, 16384], P('seg', None, 'head'), may hold values from -6 to 6
- parents: int32 [8], replicated, may hold values from -1 to 7, as said below
- levels: int32 [8], replicated, may hold values from 0 to 2, as said below
Outputs:
- outputs: bfloat16 [8, 256, 16384], P('seg', None, 'head')
- grad_inputs: bfloat16 [8, 256, 16384], P('seg', None, 'head')
- grad_deltas: float32 [8, 256, 256], P('seg', 'head')
- grad_writer: bfloat16 [8, 256, 1024], P('seg', 'head')
- grad_reader: bfloat16 [8, 256, 1024], P('seg', 'head')
Inputs may be any that keep to these rules, and one draw needn't show every extreme that they name: `parents`: roots have parent -1 and level 0; every other segment's parent has a level one less than its own. A segment has at most four children, and some segment has level 2. levels[s] is the number of ancestors of segment s.
All inputs are finite; a program needn't handle non-finite values.
Results may differ from a plain program's by a relative error of at most 0.0046.
Values may be sent and summed in bfloat16 or wider, within the bound.
No kernel may reach another device: no remote copies, remote signals or barrier semaphores. Data moves between devices by JAX's collectives and lax.ppermute only.
A program may use at most 128 MiB of HBM per device.

v0:
```python
import jax
import jax.numpy as jnp
from jax import lax
from jax.sharding import PartitionSpec as P

H = 256
P_SIZE = 64
N = 128
G = 8
BLOCK = 256
DEPTH = 3


exact_mode = lax.Precision.HIGHEST


def ssd_forward(values, deltas, rates, writer, reader, start, block):
    length, groups, per_group, width = values.shape
    state_size = writer.shape[-1]
    blocks = length // block
    log_decay = (-rates[:, :, None] * deltas).reshape(groups, per_group, blocks, block)
    within = jnp.cumsum(log_decay, axis=-1)
    value_blk = values.reshape(blocks, block, groups, per_group, width)
    write_blk = writer.reshape(blocks, block, groups, state_size)
    read_blk = reader.reshape(blocks, block, groups, state_size)
    delta_blk = deltas.reshape(groups, per_group, blocks, block)
    scores = jnp.einsum("cign,cjgn->gcij", read_blk, write_blk, precision=exact_mode)
    positions = jnp.arange(block)
    causal = positions[:, None] >= positions[None, :]
    log_gap = within[..., :, None] - within[..., None, :]
    decays = jnp.exp(jnp.where(causal, log_gap, -jnp.inf))
    weights = scores[:, None] * decays * delta_blk[..., None, :]
    within_out = jnp.einsum("ghcij,cjghp->cighp", weights, value_blk, precision=exact_mode)
    tail_decay = jnp.exp(within[..., -1:] - within) * delta_blk
    local_state = jnp.einsum(
        "ghcj,cjghp,cjgn->cghpn", tail_decay, value_blk, write_blk, precision=exact_mode
    )
    totals = jnp.exp(within[..., -1])
    current = start
    read_out = jnp.einsum("ign,ghpn->ighp", read_blk[0], current, precision=exact_mode)
    scale_in = jnp.transpose(jnp.exp(within[:, :, 0, :]), (2, 0, 1))
    outer_terms = [read_out * scale_in[..., None]]
    current = totals[:, :, 0, None, None] * current + local_state[0]
    output = within_out + jnp.stack(outer_terms)
    return (output.reshape(length, groups, per_group, width), current)


def segment_end(values, deltas, rates, writer):
    running = jnp.cumsum(-rates[:, :, None] * deltas, axis=-1)
    total = running[..., -1]
    tail_decay = jnp.exp(total[..., None] - running) * deltas
    local_state = jnp.einsum("ghj,jghp,jgn->ghpn", tail_decay, values, writer, precision=exact_mode)
    return (local_state, jnp.exp(total))


def start_grad(grads, deltas, rates, reader):
    running = jnp.cumsum(-rates[:, :, None] * deltas, axis=-1)
    return jnp.einsum("ghi,ighp,ign->ghpn", jnp.exp(running), grads, reader, precision=exact_mode)


def shards(inputs, deltas, rates, skips, writer, reader, grad_out, parents, levels):
    length = inputs.shape[1]
    heads = deltas.shape[1]
    per_group_all = H // G
    local_groups = max(1, heads // per_group_all)
    per_group = heads // local_groups
    first_group = lax.axis_index("head") * heads // per_group_all
    own_slot = lax.axis_index("seg")
    rate_grid = rates.reshape(local_groups, per_group)
    skip_grid = skips.reshape(local_groups, per_group)
    values = inputs[0].astype(jnp.float32).reshape(length, local_groups, per_group, P_SIZE)
    delta_one = deltas[0].reshape(local_groups, per_group, length)
    write_one = lax.dynamic_slice_in_dim(
        writer[0].reshape(length, G, N), first_group, local_groups, 1
    ).astype(jnp.float32)
    read_one = lax.dynamic_slice_in_dim(
        reader[0].reshape(length, G, N), first_group, local_groups, 1
    ).astype(jnp.float32)
    grads = grad_out[0].astype(jnp.float32).reshape(length, local_groups, per_group, P_SIZE)
    local_state, decay_all = segment_end(values, delta_one, rate_grid, write_one)
    start_part = start_grad(grads, delta_one, rate_grid, read_one)
    safe_parent = jnp.maximum(parents, 0)
    own_level = levels[own_slot]
    starts = jnp.zeros_like(local_state)
    for repeat in range(DEPTH - 1):
        end_state = (decay_all[..., None, None] * starts + local_state).astype(jnp.bfloat16)
        gathered = lax.all_gather(end_state[None], "seg", axis=0, tiled=True)
        starts = jnp.where(
            own_level == repeat + 1, gathered[safe_parent[own_slot]].astype(jnp.float32), starts
        )
    gathered_part, gathered_decay = (
        lax.all_gather(start_part[None], "seg", axis=0, tiled=True),
        lax.all_gather(decay_all[None], "seg", axis=0, tiled=True),
    )
    upward = parents
    carried = jnp.ones_like(gathered_decay)
    factors = jnp.zeros_like(gathered_decay)
    for repeat in range(DEPTH - 1):
        factors = factors + jnp.where((upward == own_slot)[:, None, None], carried, 0.0)
        lifted = jnp.maximum(upward, 0)
        carried = carried * gathered_decay[lifted]
        upward = jnp.where(upward < 0, -1, parents[lifted])
    grad_end = jnp.einsum("dgh,dghpn->ghpn", factors, gathered_part, precision=exact_mode)

    def core_map(values, delta_one, write_one, read_one):
        return ssd_forward(values, delta_one, rate_grid, write_one, read_one, starts, BLOCK)

    (core_out, end_state), pullback = jax.vjp(core_map, values, delta_one, write_one, read_one)
    grad_values, grad_delta, grad_write, grad_read = pullback((grads, grad_end))
    result = core_out + skip_grid[None, :, :, None] * values
    grad_values = grad_values + skip_grid[None, :, :, None] * grads
    blank = jnp.zeros((length, G, N), jnp.float32)
    padded_write = lax.dynamic_update_slice_in_dim(blank, grad_write, first_group, 1).reshape(
        length, G * N
    )
    padded_read = lax.dynamic_update_slice_in_dim(blank, grad_read, first_group, 1).reshape(
        length, G * N
    )
    summed_write, summed_read = (
        lax.psum_scatter(padded_write, "head", scatter_dimension=0, tiled=True),
        lax.psum_scatter(padded_read, "head", scatter_dimension=0, tiled=True),
    )
    return (
        result.reshape(1, length, heads * P_SIZE).astype(jnp.bfloat16),
        grad_values.reshape(1, length, heads * P_SIZE).astype(jnp.bfloat16),
        grad_delta.reshape(1, heads, length),
        summed_write.astype(jnp.bfloat16)[None],
        summed_read.astype(jnp.bfloat16)[None],
    )


def solution(mesh):
    placed = (
        P("seg", None, "head"),
        P("seg", "head", None),
        P("head"),
        P("head"),
        P("seg", None, None),
        P("seg", None, None),
        P("seg", None, "head"),
        P(),
        P(),
    )
    return jax.shard_map(
        shards,
        mesh=mesh,
        in_specs=placed,
        out_specs=(
            P("seg", None, "head"),
            P("seg", None, "head"),
            P("seg", "head", None),
            P("seg", "head", None),
            P("seg", "head", None),
        ),
        check_vma=False,
    )
```

profile of v0, /device:TPU:0, one launch (start us, length us, event | category | flops | bytes accessed | tf_op | source)
XLA Modules:
  0.0 479.3 jit_solution(16637100516355102688)
XLA Ops:
  7.2 3.3 copy.161
  13.4 3.9 add_convert_fusion.2
  17.4 4.3 copy.168
  23.0 5.6 %fusion.30 = f32[2,32,64,128]{3,2,1,0:T(8,128)} fusion(f32[256,2,32,64]{0,3,2,1:T(8,128)} %bitcast.265, f32[256,2,32]{0,2,1:T(8,128)S(1)} %get-tuple-element.16, bf16[256,8,128]{0,2,1:T(8,128)(2,1)S(1)} %bitcast.290, s32[]{:T(128)S(6)} %select_n.65), kind=kOutput, calls=%fused_computation.43 | convolution fusion | flops 1611661312 | bytes 6488068 | tf_op jit(solution)/shard_map/ghi,ighp,ign->ghpn/dot_general | solution.py:58
  32.5 69.8 %all-gather.8.cloned.1.call-done = bf16[16,32,64,128]{3,2,1,0:T(8,128)(2,1)} async-done(((bf16[2,32,64,128]{3,2,1,0:T(8,128)(2,1)}), bf16[16,32,64,128]{3,2,1,0:T(8,128)(2,1)}) %all-gather.8.cloned.1.call-update) | async-done | bytes 8388624 | tf_op jit(solution)/shard_map/all_gather | solution.py:87
  105.6 4.1 copy.173
  113.9 9.5 %all-gather.2 = f32[16,32,1]{1,2,0:T(1,128)S(1)} all-gather(f32[2,32,1]{1,2,0:T(1,128)S(1)} %bitcast.318), channel_id=4, replica_groups=mesh['seg'=8,'head'=4] {'seg'}, dimensions={0}, use_global_device_ids=true | all-gather | bytes 2304 | tf_op jit(solution)/shard_map/all_gather | solution.py:93
  130.9 123.1 %all-gather.12.cloned.1.call-done = f32[16,32,64,128]{3,2,1,0:T(8,128)} async-done(((f32[2,32,64,128]{3,2,1,0:T(8,128)}), f32[16,32,64,128]{3,2,1,0:T(8,128)}) %all-gather.12.cloned.1.call-update) | async-done | bytes 16777232 | tf_op jit(solution)/shard_map/all_gather | solution.py:92
  254.1 41.5 %fusion = f32[2,32,1,64,128]{4,2,3,1,0:T(1,128)S(1)} fusion(f32[8,2,32,1,1]{0,3,4,2,1:T(1,128)} %copy.191, f32[8,2,32,64,128]{4,3,2,1,0:T(8,128)} %bitcast.276), kind=kOutput, calls=%fused_computation.2 | convolution fusion | flops 50331648 | bytes 18876416 | tf_op jit(solution)/shard_map/dgh,dghpn->ghpn/dot_general | solution.py:103
  296.9 4.7 fusion.24
  301.6 34.4 %all-gather.10.cloned.1.call-done = bf16[16,32,64,128]{3,2,1,0:T(8,128)(2,1)} async-done(((bf16[2,32,64,128]{3,2,1,0:T(8,128)(2,1)}), bf16[16,32,64,128]{3,2,1,0:T(8,128)(2,1)}) %all-gather.10.cloned.1.call-update) | async-done | bytes 8388624 | tf_op jit(solution)/shard_map/all_gather | solution.py:87
  339.4 5.7 %fusion.28 = (f32[256,2,32]{0,2,1:T(8,128)S(1)}, f32[2,32,64,256]{3,2,1,0:T(8,128)}) fusion(f32[256,2,32,64]{0,3,2,1:T(8,128)S(1)} %bitcast.267, bf16[256,8,128]{0,2,1:T(8,128)(2,1)S(1)} %bitcast.292, s32[]{:T(128)S(6)} %select_n.65, pred[]{:T(512)} %bitcast.12, pred[]{:T(512)} %bitcast.10, bf16[8,2,32,64,128]{4,3,2,1,0:T(8,128)(2,1)} %bitcast.307, ...), kind=kOutput, calls=%fused_computation.40 | convolution fusion | flops 1614790656 | bytes 10683400 | tf_op jit(solution)/shard_map/jvp(ign,ghpn->ighp)/dot_general | solution.py:40
  350.7 13.4 %fusion.9 = (f32[2,32,256]{2,1,0:T(8,128)}, f32[2,32,256]{2,1,0:T(8,128)}, f32[2,32,256]{2,1,0:T(8,128)}, f32[2,256,256]{2,1,0:T(8,128)S(1)}) fusion(f32[2,32,256]{2,1,0:T(8,128)S(1)} %bitcast.303, f32[2,32,256]{2,1,0:T(8,128)} %copy.159, f32[2,256,256]{2,1,0:T(8,128)} %fusion.78, pred[256,256]{1,0:T(8,128)(4,1)} %iota_compare_fusion, ...), kind=kOutput, calls=%fused_computation.13 | convolution fusion | flops 591216640 | bytes 5636096 | tf_op jit(solution)/shard_map/transpose(jvp(ghcij,cjghp->cighp))/dot_general | solution.py:33
  364.1 11.8 %bitcast_add_fusion = f32[1,256,2,32,64]{1,4,3,2,0:T(8,128)} fusion(f32[2,32,64,256]{3,2,1,0:T(8,128)S(1)} %copy-done.4, bf16[2,32,64,256]{3,2,1,0:T(8,128)(2,1)S(1)} %bitcast.295, f32[2,32,256]{2,1,0:T(8,128)S(1)} %bitcast.304, f32[2,32,256]{2,1,0:T(8,128)S(1)} %copy-done.25, f32[2,256,256]{2,1,0:T(8,128)S(1)} %copy-done.17, ...), kind=kOutput, calls=%fused_computation.32 | convolution fusion | flops 3240099840 | bytes 11272192 | tf_op jit(solution)/shard_map/transpose(jvp(ghcij,cjghp->cighp))/dot_general | solution.py:33
  376.0 5.6 %copy.174 = f32[1,256,4096]{2,1,0:T(8,128)} copy(f32[1,256,4096]{1,2,0:T(8,128)} %bitcast.278) | data formatting | bytes 8388608 | tf_op jit(solution)/shard_map/transpose(jvp())/reshape | solution.py:23
  383.6 5.4 %fusion.45 = f32[256,2,128]{0,2,1:T(8,128)S(1)} fusion(f32[1,256,2,128]{1,3,2,0:T(8,128)S(1)} %convolution_bitcast_fusion.1, f32[2,32,64,128]{3,2,1,0:T(8,128)} %bitcast.275, bf16[256,2,32,64]{0,3,2,1:T(8,128)(2,1)S(1)} %bitcast.271, f32[256,2,32]{0,2,1:T(8,128)} %copy.172), kind=kOutput, calls=%fused_computation.60 | convolution fusion | flops 1612775424 | bytes 4784128 | tf_op jit(solution)/shard_map/transpose(jvp(ghcj,cjghp,cjgn->cghpn))/dot_general | solution.py:35
  389.9 6.7 %dynamic_update_slice.6 = f32[256,8,128]{2,1,0:T(8,128)S(1)} dynamic-update-slice(f32[256,8,128]{2,1,0:T(8,128)S(1)} %broadcast_in_dim.114.clone, f32[256,2,128]{2,1,0:T(2,128)} %copy.186, s32[]{:T(128)} %constant.27.clone.1, s32[]{:T(128)S(6)} %select_n.65, s32[]{:T(128)} %constant.27.clone.1) | dynamic-update-slice | bytes 524292 | tf_op jit(solution)/shard_map/dynamic_update_slice | solution.py:113
  398.0 17.4 %bitcast_add_fusion.1 = f32[1,256,2,32,64]{1,4,3,2,0:T(8,128)} fusion(f32[2,32,64,256]{3,2,1,0:T(8,128)} %get-tuple-element.27, bf16[256,2,32,64]{0,3,2,1:T(8,128)(2,1)S(1)} %bitcast.272, f32[2,32,256]{2,1,0:T(8,128)S(1)} %bitcast.305, f32[2,32,256]{2,1,0:T(8,128)} %copy.159, f32[2,256,256]{2,1,0:T(8,128)} %fusion.78, ...), kind=kOutput, calls=%fused_computation.33 | convolution fusion | flops 3240099840 | bytes 11272192 | tf_op jit(solution)/shard_map/jvp(ghcij,cjghp->cighp)/dot_general | solution.py:33
  415.4 5.8 %copy.166 = f32[1,256,4096]{2,1,0:T(8,128)} copy(f32[1,256,4096]{1,2,0:T(8,128)} %bitcast.277) | data formatting | bytes 8388608 | tf_op jit(solution)/shard_map/jvp()/reshape | solution.py:45
  423.7 5.0 %reduce-window.26 = f32[2,32,1,2,128]{4,1,2,3,0:T(8,128)S(1)} reduce-window(f32[2,32,1,2,128]{4,1,2,3,0:T(8,128)S(1)} %copy.181, f32[]{:T(128)} %constant.53.clone.1), window={size=1x1x1x1x128 pad=0_0x0_0x0_0x0_0x0_127}, to_apply=%region_10.11 | reduce-window | flops 2080768 | bytes 131076 | tf_op jit(solution)/shard_map/reduce-window.4
  430.8 6.4 %fusion.52 = f32[256,2,128]{0,2,1:T(8,128)S(1)} fusion(f32[1,256,2,128]{1,3,2,0:T(8,128)S(1)} %convolution_bitcast_fusion, f32[256,2,32,64]{0,3,2,1:T(8,128)} %bitcast.266, f32[256,2,32]{0,2,1:T(8,128)S(1)} %copy-done.19, pred[]{:T(512)} %bitcast.12, pred[]{:T(512)} %bitcast.10, bf16[8,2,32,64,128]{4,3,2,1,0:T(8,128)(2,1)} %bitcast.308, s32[]{:T(128)S(6)} %select_n.70, ...), kind=kOutput, calls=%fused_computation.65 | convolution fusion | flops 1613824000 | bytes 6882308 | tf_op jit(solution)/shard_map/transpose(jvp(ign,ghpn->ighp))/dot_general | solution.py:40
  437.4 5.6 %dynamic_update_slice.7 = f32[256,8,128]{2,1,0:T(8,128)S(1)} dynamic-update-slice(f32[256,8,128]{2,1,0:T(8,128)S(1)} %broadcast_in_dim.114.clone.1, f32[256,2,128]{2,1,0:T(2,128)S(1)} %copy.188, s32[]{:T(128)} %constant.27.clone.1, s32[]{:T(128)S(6)} %select_n.65, s32[]{:T(128)} %constant.27.clone.1) | dynamic-update-slice | bytes 524292 | tf_op jit(solution)/shard_map/dynamic_update_slice | solution.py:116
  446.3 7.7 %add_convert_fusion = (bf16[1,256,4096]{2,1,0:T(8,128)(2,1)}, bf16[1,256,4096]{2,1,0:T(8,128)(2,1)}) fusion(f32[1,256,4096]{2,1,0:T(8,128)} %copy.174, f32[4096]{0:T(1024)S(1)} %mul.211, bf16[1,256,4096]{2,1,0:T(8,128)(2,1)S(1)} %copy-done.3, f32[1,256,4096]{2,1,0:T(8,128)} %copy.166, bf16[1,256,4096]{2,1,0:T(8,128)(2,1)} %param.9), kind=kLoop, calls=%fused_computation.42 | loop fusion | flops 8388608 | bytes 16793600 | tf_op jit(solution)/shard_map/convert_element_type | solution.py:125
  455.7 15.2 %reduce-scatter.5.cloned.1.call-done = f32[64,1024]{1,0:T(8,128)} async-done(((f32[256,1024]{1,0:T(8,128)}), f32[64,1024]{1,0:T(8,128)}) %reduce-scatter.5.cloned.1.call-update) | async-done | bytes 262160 | tf_op jit(solution)/shard_map/reduce_scatter | solution.py:121
  (166 shorter events, 45.3 us)
Async XLA Ops:
  7.2 95.1 %all-gather.8.cloned.1.call-start = ((), (), s32[]{:S(2)}) async-start(), calls=%async_computation.4 | async-start | bytes 9437184 | tf_op jit(solution)/shard_map/all_gather | solution.py:87
  13.3 282.4 %copy-start.9 = (bf16[1,256,1024]{1,2,0:T(8,128)(2,1)}, bf16[1,256,1024]{1,2,0:T(8,128)(2,1)S(1)}, u32[]{:S(2)}) copy-start(bf16[1,256,1024]{1,2,0:T(8,128)(2,1)S(1)} %copy.153) | copy-start | bytes 1572868
  17.4 236.7 %all-gather.12.cloned.1.call-start = ((), (), s32[]{:S(2)}) async-start(), calls=%async_computation.6 | async-start | bytes 18874368 | tf_op jit(solution)/shard_map/all_gather | solution.py:92
  23.0 7.6 %copy-start.35 = (s32[8]{0:T(128)S(1)}, s32[8]{0:T(128)}, u32[]{:S(2)}) copy-start(s32[8]{0:T(128)} %param.17) | copy-start | bytes 100
  28.6 307.3 %all-gather.10.cloned.1.call-start = ((), (), s32[]{:S(2)}) async-start(), calls=%async_computation.5 | async-start | bytes 9437184 | tf_op jit(solution)/shard_map/all_gather | solution.py:87
  105.5 21.2 %copy-start.36 = (f32[64]{0:T(128)S(1)}, f32[64]{0:T(128)}, u32[]{:S(2)}) copy-start(f32[64]{0:T(128)} %param.12) | copy-start | bytes 772
  105.5 348.5 %reduce-scatter.3.cloned.1.call-start = ((), (), s32[]{:S(2)}) async-start(), calls=%async_computation.2 | async-start | bytes 1310720 | tf_op jit(solution)/shard_map/reduce_scatter | solution.py:120
  126.4 169.2 %copy-start.5 = (f32[2,32,1,256]{1,0,3,2:T(2,128)}, f32[2,32,1,256]{1,0,3,2:T(2,128)S(1)}, u32[]{:S(2)}) copy-start(f32[2,32,1,256]{1,0,3,2:T(2,128)S(1)} %copy.170) | copy-start | bytes 196612
  126.6 169.0 %copy-start.28 = (f32[2,32,2]{1,0,2:T(2,128)}, f32[2,32,2]{1,0,2:T(2,128)S(1)}, u32[]{:S(2)}) copy-start(f32[2,32,2]{1,0,2:T(2,128)S(1)} %copy.157) | copy-start | bytes 1540
  350.7 13.4 %copy-start.4 = (f32[2,32,64,256]{3,2,1,0:T(8,128)S(1)}, f32[2,32,64,256]{3,2,1,0:T(8,128)}, u32[]{:S(2)}) copy-start(f32[2,32,64,256]{3,2,1,0:T(8,128)} %get-tuple-element.25) | copy-start | bytes 12582916
  350.7 13.4 %copy-start.10 = (bf16[1,256,4096]{1,2,0:T(8,128)(2,1)S(1)}, bf16[1,256,4096]{1,2,0:T(8,128)(2,1)}, u32[]{:S(2)}) copy-start(bf16[1,256,4096]{1,2,0:T(8,128)(2,1)} %copy.173) | copy-start | bytes 6291460
  350.7 13.4 %copy-start.17 = (f32[2,256,256]{2,1,0:T(8,128)S(1)}, f32[2,256,256]{2,1,0:T(8,128)}, u32[]{:S(2)}) copy-start(f32[2,256,256]{2,1,0:T(8,128)} %fusion.78) | copy-start | bytes 1572868
  350.7 13.4 %copy-start.21 = (f32[256,2,32]{0,2,1:T(8,128)S(1)}, f32[256,2,32]{0,2,1:T(8,128)}, u32[]{:S(2)}) copy-start(f32[256,2,32]{0,2,1:T(8,128)} %copy.172) | copy-start | bytes 196612
  350.7 13.5 %copy-start.25 = (f32[2,32,256]{2,1,0:T(8,128)S(1)}, f32[2,32,256]{2,1,0:T(8,128)}, u32[]{:S(2)}) copy-start(f32[2,32,256]{2,1,0:T(8,128)} %copy.159) | copy-start | bytes 196612
  350.7 13.4 %copy-start.26 = (pred[256,256]{1,0:T(8,128)(4,1)S(1)}, pred[256,256]{1,0:T(8,128)(4,1)}, u32[]{:S(2)}) copy-start(pred[256,256]{1,0:T(8,128)(4,1)} %iota_compare_fusion) | copy-start | bytes 196612
  364.1 19.2 %copy-start.11 = (f32[2,256,256]{2,1,0:T(8,128)}, f32[2,256,256]{2,1,0:T(8,128)S(1)}, u32[]{:S(2)}) copy-start(f32[2,256,256]{2,1,0:T(8,128)S(1)} %get-tuple-element.8) | copy-start | bytes 1572868
  397.9 72.9 %reduce-scatter.5.cloned.1.call-start = ((), (), s32[]{:S(2)}) async-start(), calls=%async_computation.3 | async-start | bytes 1310720 | tf_op jit(solution)/shard_map/reduce_scatter | solution.py:121
  415.4 7.4 %copy-start.23 = (f32[2,32,256]{2,1,0:T(8,128)S(1)}, f32[2,32,256]{2,1,0:T(8,128)}, u32[]{:S(2)}) copy-start(f32[2,32,256]{2,1,0:T(8,128)} %get-tuple-element.6) | copy-start | bytes 196612
  415.4 7.5 %copy-start.27 = (f32[2,32,256]{2,1,0:T(8,128)S(1)}, f32[2,32,256]{2,1,0:T(8,128)}, u32[]{:S(2)}) copy-start(f32[2,32,256]{2,1,0:T(8,128)} %get-tuple-element.5) | copy-start | bytes 196612
  415.4 7.8 %copy-start.32 = (f32[2,32,1,1]{1,0,3,2:T(2,128)S(1)}, f32[2,32,1,1]{1,0,3,2:T(2,128)}, u32[]{:S(2)}) copy-start(f32[2,32,1,1]{1,0,3,2:T(2,128)} %get-tuple-element.14) | copy-start | bytes 772
  421.2 8.2 %copy-start.12 = (f32[2,256,256]{2,1,0:T(8,128)S(1)}, f32[2,256,256]{2,1,0:T(8,128)}, u32[]{:S(2)}) copy-start(f32[2,256,256]{2,1,0:T(8,128)} %copy-done.11) | copy-start | bytes 1572868
  421.2 9.6 %copy-start.19 = (f32[256,2,32]{0,2,1:T(8,128)S(1)}, f32[256,2,32]{0,2,1:T(8,128)}, u32[]{:S(2)}) copy-start(f32[256,2,32]{0,2,1:T(8,128)} %copy.165) | copy-start | bytes 196612
  437.2 7.5 %copy-start.22 = (f32[2,32,1,256]{3,1,0,2:T(8,128)S(1)}, f32[2,32,1,256]{3,1,0,2:T(8,128)}, u32[]{:S(2)}) copy-start(f32[2,32,1,256]{3,1,0,2:T(8,128)} %copy.176) | copy-start | bytes 196612
  437.2 9.1 %copy-start.3 = (bf16[1,256,4096]{2,1,0:T(8,128)(2,1)S(1)}, bf16[1,256,4096]{2,1,0:T(8,128)(2,1)}, u32[]{:S(2)}) copy-start(bf16[1,256,4096]{2,1,0:T(8,128)(2,1)} %param.15) | copy-start | bytes 6291460
  (18 other events, 82.9 us)
Sparse Core Ops, SparseCore 0:
  17.5 84.7 all-gather.7
  104.4 149.5 all-gather.11
  255.7 80.2 all-gather.9
  398.0 26.4 reduce-scatter.2
  444.4 26.3 reduce-scatter.4
where the time goes:
time: 487 us; the launch traced here: 479 us
  waiting for transfers between devices  242 us (50%)
  matrix products  119 us (24%)
  local copies, waits for them, and re-layouts  59.6 us (12%)
  other arithmetic  30.9 us (6%)
  between operations  18.1 us (4%)
  blocking collectives  9.45 us (2%)
    all_gather x1, waiting for transfers between devices, shards(): lax.all_gather(start_part[None], 'seg', axis=0, tiled=True)  123 us
    all_gather x2, waiting for transfers between devices, shards(): gathered = lax.all_gather(end_state[None], 'seg', axis=0, tiled=True)  104 us
    dot_general x3, matrix products, ssd_forward(): jnp.einsum('ghcij,cjghp->cighp', weights, value_blk, precision=exact_mode)  42.6 us
    dot_general x1, matrix products, shards(): jnp.einsum('dgh,dghpn->ghpn', factors, gathered_part, precision=exact_mode)  41.5 us
    reduce_scatter x1, waiting for transfers between devices, shards(): lax.psum_scatter(padded_read, 'head', scatter_dimension=0, tiled=True)  15.2 us
    unnamed x82, local copies, waits for them, and re-layouts  14.8 us
    dot_general x2, matrix products, ssd_forward(): jnp.einsum('ign,ghpn->ighp', read_blk[0], current, precision=exact_mode)  12.1 us
    dot_general x2, matrix products, ssd_forward(): jnp.einsum('ghcj,cjghp,cjgn->cghpn', tail_decay, value_blk, write_blk, pr...  10.1 us
  transfers between devices with their start and end apart: 5, of which 4 were waited for; matrix products, arithmetic and copies ran while one was open for 28% of the time, Pallas kernels for 0%

commit v1 on v0

v1 whole, which is shorter than its diff:
```python
import functools

import jax
import jax.numpy as jnp
from jax import lax
from jax.experimental import pallas as pl
from jax.experimental.pallas import tpu as pltpu
from jax.sharding import PartitionSpec as P

H = 256
P_SIZE = 64
N = 128
G = 8
DEPTH = 3
TILE = 256
SLOTS = 64

F32 = jnp.float32
BF16 = jnp.bfloat16


def dot(a, b, dims=((1,), (0,))):
    return lax.dot_general(a, b, (dims, ((), ())), preferred_element_type=F32)


NT = ((1,), (1,))


def split(value, parts):
    pieces = []
    for _ in range(parts):
        piece = value.astype(BF16)
        pieces.append(piece)
        value = value - piece.astype(F32)
    return pieces


def iota(shape, axis):
    return lax.broadcasted_iota(jnp.int32, shape, axis)


def onehot(cond):
    return jnp.where(cond, 1.0, 0.0).astype(BF16)


def spread(step):
    shape = (2 * SLOTS, TILE)
    head = step * (TILE // P_SIZE) + iota(shape, 1) // P_SIZE
    return onehot((iota(shape, 0) % SLOTS) == head)


def local_kernel(
    per_group,
    _,
    x_ref,
    dy_ref,
    delta_ref,
    rate_ref,
    b_ref,
    c_ref,
    u_ref,
    v_ref,
    xs_ref,
    ys_ref,
    table_ref,
    low_ref,
    up_ref,
    gb_ref,
    gc_ref,
    acc_ref,
):
    step = pl.program_id(0)
    length = x_ref.shape[0]
    square = (length, length)

    @pl.when(step == 0)
    def _():
        tri = onehot(iota(square, 0) >= iota(square, 1))
        eye = onehot(iota(square, 0) == iota(square, 1))
        pieces = split(delta_ref[...], 3)
        sums = sum(dot(tri, piece, NT) for piece in pieces)
        delta = sum(dot(eye, piece, NT) for piece in pieces)
        log = rate_ref[...] * sums
        grow = split(jnp.exp(log) * delta, 2)
        fall = split(jnp.exp(-log), 2)
        table_ref[0] = jnp.concatenate(fall, axis=1)
        table_ref[1] = jnp.concatenate(grow, axis=1)

    lanes = spread(step)
    fall = dot(table_ref[0], lanes)
    grow = dot(table_ref[1], lanes)
    xs, xs_low = split(x_ref[...].astype(F32) * grow, 2)
    ys, ys_low = split(dy_ref[...].astype(F32) * fall, 2)
    xs_ref[...] = xs
    ys_ref[...] = ys
    b, c = b_ref[...], c_ref[...]
    u = dot(b, xs, ((0,), (0,))) + dot(b, xs_low, ((0,), (0,)))
    v = dot(c, ys, ((0,), (0,))) + dot(c, ys_low, ((0,), (0,)))
    u_ref[...] = (u * fall[length - 1 :]).astype(BF16)
    v_ref[...] = v.astype(BF16)
    part = dot(ys, xs, NT)
    inner = step % per_group

    @pl.when(inner == 0)
    def _():
        acc_ref[...] = part

    @pl.when(inner > 0)
    def _():
        acc_ref[...] += part

    @pl.when(inner == per_group - 1)
    def _():
        lower = iota(square, 0) >= iota(square, 1)
        upper = iota(square, 0) <= iota(square, 1)
        low_ref[...] = jnp.where(lower, dot(c, b, NT), 0.0).astype(BF16)
        up_ref[...] = jnp.where(upper, dot(b, c, NT), 0.0).astype(BF16)
        high, low = split(jnp.where(lower, acc_ref[...], 0.0), 2)
        gc_ref[...] = dot(high, b) + dot(low, b)
        gb_ref[...] = dot(high, c, ((0,), (0,))) + dot(low, c, ((0,), (0,)))


def local_part(x, dy, delta, rate, writer, reader, first_group, local_groups):
    length, lanes = x.shape
    steps = lanes // TILE
    per_group = steps // local_groups
    tile = lambda rows: pl.BlockSpec((rows, TILE), lambda i, f: (0, i))
    whole = lambda *shape: pl.BlockSpec(shape, lambda i, f: (0,) * len(shape))
    group = lambda rows, cols: pl.BlockSpec((None, rows, cols), lambda i, f: (i // per_group, 0, 0))
    proj = pl.BlockSpec((length, N), lambda i, f: (0, f[0] + i // per_group))
    shape = jax.ShapeDtypeStruct
    return pl.pallas_call(
        functools.partial(local_kernel, per_group),
        grid_spec=pltpu.PrefetchScalarGridSpec(
            num_scalar_prefetch=1,
            grid=(steps,),
            in_specs=[
                tile(length),
                tile(length),
                whole(SLOTS, length),
                whole(1, SLOTS),
                proj,
                proj,
            ],
            out_specs=[
                tile(N),
                tile(N),
                tile(length),
                tile(length),
                whole(2, length, 2 * SLOTS),
                group(length, length),
                group(length, length),
                group(length, N),
                group(length, N),
            ],
            scratch_shapes=[pltpu.VMEM((length, length), F32)],
        ),
        out_shape=[
            shape((N, lanes), BF16),
            shape((N, lanes), BF16),
            shape((length, lanes), BF16),
            shape((length, lanes), BF16),
            shape((2, length, 2 * SLOTS), BF16),
            shape((local_groups, length, length), BF16),
            shape((local_groups, length, length), BF16),
            shape((local_groups, length, N), F32),
            shape((local_groups, length, N), F32),
        ],
        cost_estimate=pl.CostEstimate(
            flops=8 * length * lanes * length, transcendentals=0, bytes_accessed=12 * length * lanes
        ),
        name="local_part",
    )(first_group, x, dy, delta, rate, writer, reader)


def final_kernel(
    per_group,
    steps,
    _,
    x_ref,
    dy_ref,
    xs_ref,
    ys_ref,
    start_ref,
    end_ref,
    u_ref,
    table_ref,
    low_ref,
    up_ref,
    b_ref,
    c_ref,
    gb_in,
    gc_in,
    skip_ref,
    delta_ref,
    rate_ref,
    out_ref,
    dx_ref,
    gb_ref,
    gc_ref,
    dd_ref,
    sums_ref,
    accb_ref,
    accc_ref,
):
    step = pl.program_id(0)
    length = x_ref.shape[0]
    lanes = spread(step)
    fall = dot(table_ref[0], lanes)
    grow = dot(table_ref[1], lanes)
    xs, ys, start = xs_ref[...], ys_ref[...], start_ref[...]
    total = fall[length - 1 :]
    end = end_ref[...].astype(F32) * total
    end_high, end_low = split(end, 2)
    core = dot(low_ref[...], xs) + dot(c_ref[...], start)
    grad = dot(up_ref[...], ys) + dot(b_ref[...], end_high) + dot(b_ref[...], end_low)
    skip = skip_ref[...]
    out_ref[...] = (fall * core + skip * x_ref[...].astype(F32)).astype(out_ref.dtype)
    dx_ref[...] = (grow * grad + skip * dy_ref[...].astype(F32)).astype(dx_ref.dtype)

    inner = step % per_group

    @pl.when(inner == 0)
    def _():
        accb_ref[...] = gb_in[...]
        accc_ref[...] = gc_in[...]

    accc_ref[...] += dot(ys, start, NT)
    accb_ref[...] += dot(xs, end_high, NT) + dot(xs, end_low, NT)

    @pl.when(inner == per_group - 1)
    def _():
        gb_ref[...] = accb_ref[...].astype(gb_ref.dtype)
        gc_ref[...] = accc_ref[...].astype(gc_ref.dtype)

    direct = xs.astype(F32) * grad
    through = ys.astype(F32) * core - direct
    shape = (TILE, 2 * SLOTS)
    column = iota(shape, 1)
    head = step * (TILE // P_SIZE) + iota(shape, 0) // P_SIZE
    pick_through = onehot(column == head)
    pick_direct = onehot(column == head + SLOTS)
    high, low = split(through, 2)
    dhigh, dlow = split(direct, 2)
    rows = dot(high, pick_through) + dot(low, pick_through)
    rows = rows + dot(dhigh, pick_direct) + dot(dlow, pick_direct)

    @pl.when(step == 0)
    def _():
        sums_ref[...] = rows

    @pl.when(step > 0)
    def _():
        sums_ref[...] += rows

    held = u_ref[...].astype(F32) / total + start.astype(F32)
    last = jnp.sum(end * held, axis=0, keepdims=True)
    at_last = jnp.where(iota((8, TILE), 0) == 7, last, 0.0)
    high, low = split(at_last, 2)
    sums_ref[length - 8 :, :] += dot(high, pick_through) + dot(low, pick_through)

    @pl.when(step == steps - 1)
    def _():
        both = sums_ref[...].T
        square = (length, length)
        later = onehot(iota(square, 0) >= iota(square, 1))
        back = sum(dot(piece, later) for piece in split(both[:SLOTS], 3))
        dd_ref[...] = both[SLOTS:] / delta_ref[...] - rate_ref[...] * back


def final_part(
    x, dy, xs, ys, start, end, u, table, low, up, gb, gc, skip, delta, rate, writer, reader, first_group, grad_dtype
):
    length, lanes = x.shape
    steps = lanes // TILE
    local_groups = low.shape[0]
    per_group = steps // local_groups
    tile = lambda rows: pl.BlockSpec((rows, TILE), lambda i, f: (0, i))
    whole = lambda *shape: pl.BlockSpec(shape, lambda i, f: (0,) * len(shape))
    group = lambda rows, cols: pl.BlockSpec((None, rows, cols), lambda i, f: (i // per_group, 0, 0))
    proj = pl.BlockSpec((length, N), lambda i, f: (0, f[0] + i // per_group))
    shape = jax.ShapeDtypeStruct
    return pl.pallas_call(
        functools.partial(final_kernel, per_group, steps),
        grid_spec=pltpu.PrefetchScalarGridSpec(
            num_scalar_prefetch=1,
            grid=(steps,),
            in_specs=[
                tile(length),
                tile(length),
                tile(length),
                tile(length),
                tile(N),
                tile(N),
                tile(N),
                whole(2, length, 2 * SLOTS),
                group(length, length),
                group(length, length),
                proj,
                proj,
                group(length, N),
                group(length, N),
                tile(1),
                whole(SLOTS, length),
                whole(SLOTS, 1),
            ],
            out_specs=[
                tile(length),
                tile(length),
                pl.BlockSpec((length, N), lambda i, f: (0, i // per_group)),
                pl.BlockSpec((length, N), lambda i, f: (0, i // per_group)),
                whole(SLOTS, length),
            ],
            scratch_shapes=[
                pltpu.VMEM((length, 2 * SLOTS), F32),
                pltpu.VMEM((length, N), F32),
                pltpu.VMEM((length, N), F32),
            ],
        ),
        out_shape=[
            shape((length, lanes), BF16),
            shape((length, lanes), BF16),
            shape((length, local_groups * N), grad_dtype),
            shape((length, local_groups * N), grad_dtype),
            shape((SLOTS, length), F32),
        ],
        cost_estimate=pl.CostEstimate(
            flops=12 * length * lanes * length, transcendentals=0, bytes_accessed=16 * length * lanes
        ),
        name="final_part",
    )(
        first_group, x, dy, xs, ys, start, end, u, table, low, up, writer, reader, gb, gc, skip, delta, rate
    )


def tree_states(u, v, decay, parents, levels):
    segs = lax.axis_size("seg")
    lanes = u.shape[1]
    chunk = lanes // segs

    def spread_heads(state):
        parts = jnp.swapaxes(state.reshape(N, segs, chunk), 0, 1)
        return lax.all_to_all(parts, "seg", 0, 0)

    decay_all = lax.all_to_all(decay.reshape(segs, chunk), "seg", 0, 0)[:, None, :]
    u_all = spread_heads(u)
    v_all = spread_heads(v).astype(F32)
    safe = jnp.maximum(parents, 0)
    starts = jnp.zeros_like(u_all)
    for repeat in range(DEPTH - 1):
        ends = (decay_all * starts.astype(F32) + u_all.astype(F32)).astype(BF16)
        starts = jnp.where((levels == repeat + 1)[:, None, None], ends[safe], starts)
    link = (parents[None, :] == jnp.arange(segs)[:, None]).astype(F32)
    grad_end = jnp.zeros_like(v_all)
    for repeat in range(DEPTH - 1):
        lifted = decay_all * grad_end + v_all
        grad_end = sum(link[:, c, None, None] * lifted[c][None] for c in range(segs))

    def gather_heads(state):
        parts = lax.all_to_all(state, "seg", 0, 0)
        return jnp.swapaxes(parts, 0, 1).reshape(N, lanes)

    return gather_heads(starts), gather_heads(grad_end.astype(BF16))


def group_grads(gb, gc, members):
    shards_ = lax.axis_size("head")
    both = jnp.stack([gb, gc])
    length, width = gb.shape
    parts = both.reshape(2, shards_, length // shards_, width)
    parts = lax.all_to_all(parts, "head", 1, 1)
    if members > 1:
        parts = parts.reshape(2, shards_ // members, members, length // shards_, width).sum(2)
    parts = jnp.swapaxes(parts, 1, 2).reshape(2, length // shards_, -1)
    return parts.astype(BF16)


def shards(inputs, deltas, rates, skips, writer, reader, grad_out, parents, levels):
    heads = deltas.shape[1]
    per_group_all = H // G
    local_groups = max(1, heads // per_group_all)
    members = max(1, per_group_all // heads)
    first_group = (lax.axis_index("head") * heads // per_group_all).astype(jnp.int32)[None]
    x, dy = inputs[0], grad_out[0]
    pad = SLOTS - heads
    delta = jnp.pad(deltas[0], ((0, pad), (0, 0)))
    rate = jnp.pad(rates, (0, pad))
    u, v, xs, ys, table, low, up, gb, gc = local_part(
        x, dy, delta, rate[None, :], writer[0], reader[0], first_group, local_groups
    )
    decay = jnp.repeat(jnp.exp(-rates * jnp.sum(deltas[0], axis=1)), P_SIZE)
    start, end = tree_states(u, v, decay, parents, levels)
    out, dx, gb, gc, dd = final_part(
        x,
        dy,
        xs,
        ys,
        start,
        end,
        u,
        table,
        low,
        up,
        gb,
        gc,
        jnp.repeat(skips, P_SIZE)[None, :],
        delta,
        rate[:, None],
        writer[0],
        reader[0],
        first_group,
        BF16 if members == 1 else F32,
    )
    grads = group_grads(gb, gc, members)
    return (out[None], dx[None], dd[None, :heads], grads[0][None], grads[1][None])


def solution(mesh):
    placed = (
        P("seg", None, "head"),
        P("seg", "head", None),
        P("head"),
        P("head"),
        P("seg", None, None),
        P("seg", None, None),
        P("seg", None, "head"),
        P(),
        P(),
    )
    return jax.shard_map(
        shards,
        mesh=mesh,
        in_specs=placed,
        out_specs=(
            P("seg", None, "head"),
            P("seg", None, "head"),
            P("seg", "head", None),
            P("seg", "head", None),
            P("seg", "head", None),
        ),
        check_vma=False,
    )
```

time: 487 us -> 198 us (0.41); the launches traced: 479 us -> 197 us
  waiting for transfers between devices: 242 us -> 97 us
  matrix products: 119 us -> 0 us
  local copies, waits for them, and re-layouts: 59.6 us -> 14.6 us
  Pallas kernels: 0 us -> 41.7 us
  starting transfers between devices: 0.21 us -> 22.9 us
  other arithmetic: 30.9 us -> 11.1 us
  between operations: 18.1 us -> 0.83 us
    all_gather x3 -> x0, waiting for transfers between devices: 227 us -> none  [the longest x1 123 us: shards(): lax.all_gather(start_part[None], 'seg', axis=0, tiled=True)]
    dot_general x13 -> x0, matrix products: 119 us -> none  [the longest x3 42.6 us: ssd_forward(): jnp.einsum('ghcij,cjghp->cighp', weights, value_blk, precision=exact_mode)]
    all_to_all x0 -> x5, waiting for transfers between devices: none -> 97 us  [the longest x2 51.9 us: spread_heads(): return lax.all_to_all(parts, 'seg', 0, 0)]
    pallas_call x0 -> x2, Pallas kernels: none -> 41.7 us  [the longest x1 24.6 us: final_part(): pl.pallas_call(functools.partial(final_kernel, per_group, steps), grid_sp...]
    all_to_all x0 -> x5, starting transfers between devices: none -> 22.9 us  [the longest x2 8.66 us: spread_heads(): return lax.all_to_all(parts, 'seg', 0, 0)]
    reduce_scatter x2 -> x0, waiting for transfers between devices: 15.2 us -> none  [the longest x1 15.2 us: shards(): lax.psum_scatter(padded_read, 'head', scatter_dimension=0, tiled=True)]
    unnamed x82 -> x14, local copies, waits for them, and re-layouts: 14.8 us -> 0.06 us
    dynamic_update_slice x2 -> x0, local copies, waits for them, and re-layouts: 12.3 us -> none  [the longest x1 6.73 us: shards(): lax.dynamic_update_slice_in_dim(blank, grad_write, first_group, 1)]
  transfers between devices with their start and end apart: 5 -> 5, of which waited for: 4 -> 4; matrix products, arithmetic and copies ran while one was open for 28% -> 6% of each run, Pallas kernels for 0% -> 9%
where the time goes in v1:
time: 198 us; the launch traced here: 197 us
  waiting for transfers between devices  97 us (49%)
  Pallas kernels  41.7 us (21%)
  starting transfers between devices  22.9 us (12%)
  local copies, waits for them, and re-layouts  14.6 us (7%)
  other arithmetic  11.1 us (6%)
  blocking collectives  9.24 us (5%)
    all_to_all x2, waiting for transfers between devices, spread_heads(): return lax.all_to_all(parts, 'seg', 0, 0)  51.9 us
    all_to_all x2, waiting for transfers between devices, gather_heads(): parts = lax.all_to_all(state, 'seg', 0, 0)  45.1 us
    pallas_call x1, Pallas kernels, final_part(): pl.pallas_call(functools.partial(final_kernel, per_group, steps), grid_sp...  24.6 us
    pallas_call x1, Pallas kernels, local_part(): pl.pallas_call(functools.partial(local_kernel, per_group), grid_spec=pltp...  17.1 us
    all_to_all x1, blocking collectives, group_grads(): parts = lax.all_to_all(parts, 'head', 1, 1)  9.24 us
    all_to_all x2, starting transfers between devices, spread_heads(): return lax.all_to_all(parts, 'seg', 0, 0)  8.66 us
    all_to_all x2, starting transfers between devices, gather_heads(): parts = lax.all_to_all(state, 'seg', 0, 0)  7.93 us
    all_to_all x1, starting transfers between devices, tree_states(): lax.all_to_all(decay.reshape(segs, chunk), 'seg', 0, 0)[:, None, :]  6.35 us
  transfers between devices with their start and end apart: 5, of which 4 were waited for; matrix products, arithmetic and copies ran while one was open for 6% of the time, Pallas kernels for 9%

profile of v1, /device:TPU:0, one launch (start us, length us, event | category | flops | bytes accessed | tf_op | source)
XLA Modules:
  0.0 197.4 jit_solution(2324876334271631494)
XLA Ops:
  3.1 6.4 %all-to-all-start = ((f32[8,1,512]{2,1,0:T(1,128)}), f32[8,1,512]{2,1,0:T(1,128)S(1)}, u32[]{:S(2)}, u32[]{:S(2)}) async-start(f32[8,1,512]{2,1,0:T(1,128)} %all_to_all.21), calls=%async_computation | async-start | bytes 32768 | tf_op jit(solution)/shard_map/all_to_all | solution.py:345
  9.5 17.1 %local_part.1 = (bf16[128,4096]{1,0:T(8,128)(2,1)}, bf16[128,4096]{1,0:T(8,128)(2,1)}, bf16[256,4096]{1,0:T(8,128)(2,1)}, bf16[256,4096]{1,0:T(8,128)(2,1)}, bf1...) custom-call(s32[1]{0:T(128)} %bitcast._, ...), custom_call_target="tpu_custom_call" | custom-call | flops 2147483648 | bytes 12582912 | tf_op jit(solution)/shard_map/local_part/pallas_call | solution.py:132
  26.6 2.4 %copy.53 = bf16[16,8,8,512]{3,2,0,1:T(8,128)(2,1)} copy(bf16[16,8,8,512]{3,2,1,0:T(8,128)(2,1)} %bitcast.98) | data formatting | bytes 2097152 | tf_op jit(solution)/shard_map/reshape | solution.py:342
  28.9 5.1 %all-to-all-start.1 = ((bf16[8,128,512]{2,1,0:T(8,128)(2,1)}), bf16[8,128,512]{2,1,0:T(8,128)(2,1)S(1)}, u32[]{:S(2)}, u32[]{:S(2)}) async-start(bf16[8,128,512]{2,1,0:T(8,128)(2,1)} %bitcast.95), calls=%async_computation.1 | async-start | bytes 2097152 | tf_op jit(solution)/shard_map/all_to_all | solution.py:343
  34.1 1.1 copy.52
  35.1 25.5 %all-to-all-done.1 = bf16[8,128,512]{2,1,0:T(8,128)(2,1)S(1)} async-done(((bf16[8,128,512]{2,1,0:T(8,128)(2,1)}), bf16[8,128,512]{2,1,0:T(8,128)(2,1)S(1)}, u32[]{:S(2)}, u32[]{:S(2)}) %all-to-all-start.1) | async-done | bytes 1048608 | tf_op jit(solution)/shard_map/all_to_all | solution.py:343
  60.6 3.6 %all-to-all-start.3 = ((bf16[8,128,512]{2,1,0:T(8,128)(2,1)}), bf16[8,128,512]{2,1,0:T(8,128)(2,1)S(1)}, u32[]{:S(2)}, u32[]{:S(2)}) async-start(bf16[8,128,512]{2,1,0:T(8,128)(2,1)} %bitcast.93), calls=%async_computation.3 | async-start | bytes 2097152 | tf_op jit(solution)/shard_map/all_to_all | solution.py:343
  64.2 26.4 %all-to-all-done.3 = bf16[8,128,512]{2,1,0:T(8,128)(2,1)S(1)} async-done(((bf16[8,128,512]{2,1,0:T(8,128)(2,1)}), bf16[8,128,512]{2,1,0:T(8,128)(2,1)S(1)}, u32[]{:S(2)}, u32[]{:S(2)}) %all-to-all-start.3) | async-done | bytes 1048608 | tf_op jit(solution)/shard_map/all_to_all | solution.py:343
  90.7 2.1 %convert_add_fusion.1 = (f32[8,128,512]{2,1,0:T(8,128)}, bf16[8,128,512]{2,1,0:T(8,128)(2,1)}) fusion(bf16[8,128,512]{2,1,0:T(8,128)(2,1)S(1)} %all-to-all-done.3, f32[8,512]{1,0:T(8,128)S(1)} %broadcast_multiply_fusion, bf16[8,128,512]{2,1,0:T(8,128)(2,1)S(1)} %all-to-all-done.1), kind=kLoop, calls=%fused_computation.3 | loop fusion | flops 2621440 | bytes 5259264 | tf_op jit(solution)/shard_map/add | solution.py:356
  92.8 1.8 gather_fusion
  94.6 1.5 fusion.1
  96.1 1.8 gather_fusion.1
  97.9 1.2 broadcast_select_fusion.1
  99.1 4.4 %all-to-all-start.2 = ((bf16[8,128,512]{2,1,0:T(8,128)(2,1)}), bf16[8,128,512]{2,1,0:T(8,128)(2,1)}, u32[]{:S(2)}, u32[]{:S(2)}) async-start(bf16[8,128,512]{2,1,0:T(8,128)(2,1)} %broadcast_select_fusion.1), calls=%async_computation.2 | async-start | bytes 2097152 | tf_op jit(solution)/shard_map/all_to_all | solution.py:360
  103.7 1.5 convert_add_fusion
  105.4 2.2 %add_convert_fusion = bf16[8,128,512]{2,1,0:T(8,128)(2,1)} fusion(f32[128,512]{1,0:T(8,128)S(1)} %get-tuple-element.34, f32[128,512]{1,0:T(8,128)S(1)} %get-tuple-element.35, f32[128,512]{1,0:T(8,128)S(1)} %get-tuple-element.36, f32[128,512]{1,0:T(8,128)S(1)} %get-tuple-element.37, f32[128,512]{1,0:T(8,128)S(1)} %get-tuple-element.38, ...), kind=kLoop, calls=%fused_computation.8 | loop fusion | flops 8388608 | bytes 3145984 | tf_op jit(solution)/shard_map/convert_element_type | solution.py:363
  107.6 22.4 %all-to-all-done.2 = bf16[8,128,512]{2,1,0:T(8,128)(2,1)} async-done(((bf16[8,128,512]{2,1,0:T(8,128)(2,1)}), bf16[8,128,512]{2,1,0:T(8,128)(2,1)}, u32[]{:S(2)}, u32[]{:S(2)}) %all-to-all-start.2) | async-done | bytes 1048608 | tf_op jit(solution)/shard_map/all_to_all | solution.py:360
  130.0 3.6 %all-to-all-start.4 = ((bf16[8,128,512]{2,1,0:T(8,128)(2,1)}), bf16[8,128,512]{2,1,0:T(8,128)(2,1)S(1)}, u32[]{:S(2)}, u32[]{:S(2)}) async-start(bf16[8,128,512]{2,1,0:T(8,128)(2,1)} %add_convert_fusion), calls=%async_computation.4 | async-start | bytes 2097152 | tf_op jit(solution)/shard_map/all_to_all | solution.py:360
  135.1 2.3 %copy.43 = bf16[8,16,8,512]{3,2,0,1:T(8,128)(2,1)} copy(bf16[8,16,8,512]{3,2,1,0:T(8,128)(2,1)} %bitcast.51) | data formatting | bytes 2097152 | tf_op jit(solution)/shard_map/reshape | solution.py:361
  137.4 22.7 %all-to-all-done.4 = bf16[8,128,512]{2,1,0:T(8,128)(2,1)S(1)} async-done(((bf16[8,128,512]{2,1,0:T(8,128)(2,1)}), bf16[8,128,512]{2,1,0:T(8,128)(2,1)S(1)}, u32[]{:S(2)}, u32[]{:S(2)}) %all-to-all-start.4) | async-done | bytes 1048608 | tf_op jit(solution)/shard_map/all_to_all | solution.py:360
  160.1 1.1 copy.44
  161.2 24.6 %final_part.1 = (bf16[256,4096]{1,0:T(8,128)(2,1)}, bf16[256,4096]{1,0:T(8,128)(2,1)}, bf16[256,256]{1,0:T(8,128)(2,1)}, bf16[256,256]{1,0:T(8,128)(2,1)}, f32[64,256]{1,0:T(8,128)}) custom-call(s32[1]{0:T(128)} %bitcast._, bf16[256,4096]{1,0:T(8,128)(2,1)} %bitcast.102, bf16[256,4096]{1,0:T(8,128)(2,1)} %bitcast.104, ...), custom_call_target="tpu_custom_call" | custom-call | flops 3221225472 | bytes 16777216 | tf_op jit(solution)/shard_map/final_part/pallas_call | solution.py:283
  185.8 1.0 pad_maximum_fusion
  186.8 9.2 %all_to_all.34 = bf16[2,4,64,256]{3,2,0,1:T(8,128)(2,1)S(1)} all-to-all(bf16[2,4,64,256]{3,2,0,1:T(8,128)(2,1)S(1)} %pad_maximum_fusion), channel_id=1, replica_groups=mesh['seg'=8,'head'=4] {'head'}, dimensions={1} | all-to-all | bytes 524288 | tf_op jit(solution)/shard_map/all_to_all | solution.py:371
  (33 shorter events, 5.8 us)
Async XLA Ops:
  3.1 25.8 %all-to-all-start = ((f32[8,1,512]{2,1,0:T(1,128)}), f32[8,1,512]{2,1,0:T(1,128)S(1)}, u32[]{:S(2)}, u32[]{:S(2)}) async-start(f32[8,1,512]{2,1,0:T(1,128)} %all_to_all.21), calls=%async_computation | async-start | bytes 32768 | tf_op jit(solution)/shard_map/all_to_all | solution.py:345
  26.5 7.5 %copy-start.1 = (bf16[128,4096]{1,0:T(8,128)(2,1)S(1)}, bf16[128,4096]{1,0:T(8,128)(2,1)}, u32[]{:S(2)}) copy-start(bf16[128,4096]{1,0:T(8,128)(2,1)} %get-tuple-element.22) | copy-start | bytes 3145732
  28.9 31.7 %all-to-all-start.1 = ((bf16[8,128,512]{2,1,0:T(8,128)(2,1)}), bf16[8,128,512]{2,1,0:T(8,128)(2,1)S(1)}, u32[]{:S(2)}, u32[]{:S(2)}) async-start(bf16[8,128,512]{2,1,0:T(8,128)(2,1)} %bitcast.95), calls=%async_computation.1 | async-start | bytes 2097152 | tf_op jit(solution)/shard_map/all_to_all | solution.py:343
  34.0 30.1 %copy-start.4 = (s32[8]{0:T(128)S(1)}, s32[8]{0:T(128)}, u32[]{:S(2)}) copy-start(s32[8]{0:T(128)} %param.16) | copy-start | bytes 100
  34.1 30.2 %copy-start.5 = (s32[8]{0:T(128)S(1)}, s32[8]{0:T(128)}, u32[]{:S(2)}) copy-start(s32[8]{0:T(128)} %param.17) | copy-start | bytes 100
  60.6 30.1 %all-to-all-start.3 = ((bf16[8,128,512]{2,1,0:T(8,128)(2,1)}), bf16[8,128,512]{2,1,0:T(8,128)(2,1)S(1)}, u32[]{:S(2)}, u32[]{:S(2)}) async-start(bf16[8,128,512]{2,1,0:T(8,128)(2,1)} %bitcast.93), calls=%async_computation.3 | async-start | bytes 2097152 | tf_op jit(solution)/shard_map/all_to_all | solution.py:343
  99.1 4.5 %copy-start = (f32[8,128,512]{2,1,0:T(8,128)S(1)}, f32[8,128,512]{2,1,0:T(8,128)}, u32[]{:S(2)}) copy-start(f32[8,128,512]{2,1,0:T(8,128)} %get-tuple-element.51) | copy-start | bytes 6291460
  99.1 30.9 %all-to-all-start.2 = ((bf16[8,128,512]{2,1,0:T(8,128)(2,1)}), bf16[8,128,512]{2,1,0:T(8,128)(2,1)}, u32[]{:S(2)}, u32[]{:S(2)}) async-start(bf16[8,128,512]{2,1,0:T(8,128)(2,1)} %broadcast_select_fusion.1), calls=%async_computation.2 | async-start | bytes 2097152 | tf_op jit(solution)/shard_map/all_to_all | solution.py:360
  105.4 28.2 %copy-start.2 = (f32[64]{0:T(128)S(1)}, f32[64]{0:T(128)}, u32[]{:S(2)}) copy-start(f32[64]{0:T(128)} %param.12) | copy-start | bytes 772
  105.4 29.0 %copy-start.3 = (f32[64]{0:T(128)S(1)}, f32[64]{0:T(128)}, u32[]{:S(2)}) copy-start(f32[64]{0:T(128)} %param.11) | copy-start | bytes 772
  130.0 30.1 %all-to-all-start.4 = ((bf16[8,128,512]{2,1,0:T(8,128)(2,1)}), bf16[8,128,512]{2,1,0:T(8,128)(2,1)S(1)}, u32[]{:S(2)}, u32[]{:S(2)}) async-start(bf16[8,128,512]{2,1,0:T(8,128)(2,1)} %add_convert_fusion), calls=%async_computation.4 | async-start | bytes 2097152 | tf_op jit(solution)/shard_map/all_to_all | solution.py:360
